TPU v7x, 32 devices: a whole 2x2x4 slice. The times are simulated.
32 devices in a mesh: blk: 8 (over z, x), lay: 4 (over y, core).
Axes of the slice: x: 2, y: 2, z: 4, core: 2. Of those that a mesh axis runs over, the one named last changes fastest.
Arguments:
- three_centre: bfloat16 [512, 512, 512], P('blk', 'lay'), may hold values from -224 to 224, as said below
- metric: bfloat16 [512, 64], P('blk'), may hold values from -2 to 6
- tile_pattern: int32 [512, 16, 16], P('blk'), may hold values from 0 to 1, as said below
- density: bfloat16 [512, 512], P('lay'), may hold values from -0.00048828125 to 0.00048828125
- dens_pattern: int32 [16, 16], replicated, may hold values 0 or 1
Outputs:
- exchange: float32 [512, 512], P('lay')
Inputs may be any that keep to these rules, and one draw needn't show every extreme that they name: three_centre(P, mu, lambda) equals three_centre(P, lambda, mu). `tile_pattern`: symmetric in its last two dimensions; diagonal tiles are 1; the share of ones is drawn per group of 64 consecutive functions.
All inputs are finite; a program needn't handle non-finite values.
Results may differ from a plain program's by a relative error of at most 0.0043.
Values may be sent and summed in bfloat16 or wider, within the bound.
No kernel may reach another device: no remote copies, remote signals or barrier semaphores. Data moves between devices by JAX's collectives and lax.ppermute only.
A program may use at most 128 MiB of HBM per device.

v0:
```python
import jax
import jax.numpy as jnp
from jax import lax
from jax.sharding import PartitionSpec as P

TILE = 32


def density_adder(left_side, dens_pattern, segment):
    count = segment.shape[0]
    block_ids = jnp.arange(count, dtype=jnp.int32) // TILE
    row_pattern = jnp.take(dens_pattern, block_ids, axis=0)
    dens_mask = jnp.repeat(row_pattern, TILE, axis=1)
    kept = jnp.where(dens_mask > 0, segment, jnp.zeros_like(segment))
    return jnp.dot(left_side, kept, preferred_element_type=jnp.float32)


def per_device(three_centre, metric, tile_pattern, density, dens_pattern):
    group_size = three_centre.shape[0]
    row_count = three_centre.shape[1]
    ao_width = three_centre.shape[2]
    layers = lax.axis_size("lay")
    row_start = lax.axis_index("lay") * row_count
    row_blocks = (row_start + jnp.arange(row_count, dtype=jnp.int32)) // TILE
    pattern_rows = jnp.take(tile_pattern, row_blocks, axis=1)
    tile_mask = jnp.repeat(pattern_rows, TILE, axis=2)
    masked = jnp.where(tile_mask > 0, three_centre, jnp.zeros_like(three_centre))
    coeffs = jnp.einsum("pq,qmn->pmn", metric, masked, preferred_element_type=jnp.float32).astype(
        jnp.bfloat16
    )
    left_side = coeffs.reshape(group_size * row_count, ao_width)
    inter = density_adder(
        left_side, dens_pattern, lax.all_gather(density, "lay", axis=0, tiled=True)
    )
    column_count = ao_width // layers
    inter = inter.astype(jnp.bfloat16).reshape(group_size, row_count, layers, column_count)
    outgoing = jnp.transpose(inter, (2, 1, 0, 3)).reshape(
        layers, row_count, group_size * column_count
    )
    moved = lax.all_to_all(outgoing, "lay", split_axis=0, concat_axis=1, tiled=True)
    moved = moved.reshape(ao_width, group_size * column_count)
    partial_value = jnp.dot(
        moved, coeffs.reshape(group_size * row_count, ao_width), preferred_element_type=jnp.float32
    )
    row_sums = lax.psum_scatter(partial_value, "lay", scatter_dimension=0, tiled=True)
    return lax.psum(row_sums, "blk")


def solution(mesh):
    return jax.shard_map(
        per_device,
        mesh=mesh,
        in_specs=(P("blk", "lay", None), P("blk", None), P("blk", None, None), P("lay", None), P()),
        out_specs=P("lay", None),
        check_vma=False,
    )
```

profile of v0, /device:TPU:0, one launch (start us, length us, event | category | flops | bytes accessed | tf_op | source)
XLA Modules:
  0.0 340.7 jit_solution(9691291641924943559)
XLA Ops:
  6.5 0.0 copy-start
  6.5 0.0 reduce-scatter.2.cloned.1.call-start
  6.6 1.0 copy.28
  7.7 1.7 gather_fusion.1
  9.4 0.1 copy.27
  9.5 8.7 %all_gather.3 = bf16[512,512]{0,1:T(8,128)(2,1)S(1)} all-gather(bf16[128,512]{0,1:T(8,128)(2,1)S(1)} %copy.28), channel_id=1, replica_groups=mesh['blk'=8,'lay'=4] {'lay'}, dimensions={0}, use_global_device_ids=true | all-gather | bytes 655360 | tf_op jit(solution)/shard_map/all_gather | solution.py:33
  18.2 0.0 copy-done
  18.2 0.8 gather_fusion
  18.9 0.3 fusion
  19.2 0.7 copy.23
  19.9 11.9 %copy.24 = bf16[64,128,512]{1,2,0:T(8,128)(2,1)} copy(bf16[64,128,512]{2,1,0:T(8,128)(2,1)} %param.5) | data formatting | bytes 16777216 | tf_op args[0]
  31.9 7.5 %bitcast_select_fusion = bf16[64,128,512]{1,2,0:T(8,128)(2,1)} fusion(bf16[64,128,512]{1,2,0:T(8,128)(2,1)} %copy.24, pred[64,128,16]{1,2,0:T(8,128)(4,1)S(1)} %copy.23), kind=kLoop, calls=%fused_computation.2 | loop fusion | flops 4194304 | bytes 16908288 | tf_op jit(solution)/shard_map/jit(_where)/select_n | solution.py:27
  39.4 0.0 copy-start.2
  39.4 12.6 %copy.25 = bf16[64,128,512]{2,0,1:T(8,128)(2,1)} copy(bf16[64,128,512]{1,2,0:T(8,128)(2,1)} %bitcast_select_fusion) | data formatting | bytes 16777216 | tf_op jit(solution)/shard_map/jit(_where)/select_n | solution.py:27
  52.0 0.0 copy-done.2
  52.0 8.9 %convert_bitcast_fusion = bf16[64,128,512]{2,0,1:T(8,128)(2,1)} fusion(bf16[64,128,512]{2,0,1:T(8,128)(2,1)} %copy.25, bf16[64,64]{1,0:T(8,128)(2,1)S(1)} %copy-done.2), kind=kOutput, calls=%fused_computation.4 | convolution fusion | flops 541065216 | bytes 16785408 | tf_op jit(solution)/shard_map/pq,qmn->pmn/dot_general | solution.py:28
  60.9 11.3 %copy.26 = bf16[64,128,512]{2,1,0:T(8,128)(2,1)} copy(bf16[64,128,512]{2,0,1:T(8,128)(2,1)} %convert_bitcast_fusion) | data formatting | bytes 16777216 | tf_op jit(solution)/shard_map/convert_element_type | solution.py:28
  72.2 0.1 bitcast_select_fusion.1
  72.3 10.2 %convolution_convert_fusion = bf16[8192,512]{1,0:T(8,128)(2,1)} fusion(bf16[8192,512]{1,0:T(8,128)(2,1)} %bitcast.25, bf16[512,512]{0,1:T(8,128)(2,1)S(1)} %bitcast_select_fusion.1), kind=kOutput, calls=%fused_computation.3 | convolution fusion | flops 4299161600 | bytes 17301504 | tf_op jit(solution)/shard_map/dot_general | solution.py:15
  82.5 12.5 %reshape.138 = bf16[64,128,4,128]{3,2,1,0:T(4,128)(2,1)} reshape(bf16[8192,512]{1,0:T(8,128)(2,1)} %convolution_convert_fusion) | data formatting | bytes 16777216 | tf_op jit(solution)/shard_map/reshape | solution.py:36
  95.0 13.6 %copy.29 = bf16[64,128,4,128]{1,3,0,2:T(8,128)(2,1)} copy(bf16[64,128,4,128]{3,2,1,0:T(4,128)(2,1)} %reshape.138) | data formatting | bytes 16777216 | tf_op jit(solution)/shard_map/reshape | solution.py:36
  108.7 100.6 %all_to_all.4 = bf16[4,128,8192]{1,2,0:T(8,128)(2,1)} all-to-all(bf16[4,128,8192]{1,2,0:T(8,128)(2,1)} %bitcast.24), channel_id=1, replica_groups=mesh['blk'=8,'lay'=4] {'lay'}, dimensions={0} | all-to-all | bytes 16777216 | tf_op jit(solution)/shard_map/all_to_all | solution.py:40
  209.2 12.0 %copy.30 = bf16[4,128,8192]{2,1,0:T(8,128)(2,1)} copy(bf16[4,128,8192]{1,2,0:T(8,128)(2,1)} %all_to_all.4) | data formatting | bytes 16777216 | tf_op jit(solution)/shard_map/all_to_all | solution.py:40
  221.2 0.0 copy-start.1
  221.2 11.3 %fusion.6 = f32[512,512]{1,0:T(8,128)} fusion(bf16[512,8192]{1,0:T(8,128)(2,1)} %bitcast.27, bf16[8192,512]{1,0:T(8,128)(2,1)} %bitcast.26), kind=kOutput, calls=%fused_computation.38 | convolution fusion | flops 4294967296 | bytes 17825792 | tf_op jit(solution)/shard_map/dot_general | solution.py:42
  232.5 0.0 reduce-scatter.2.cloned.1.call-update
  232.5 0.0 all-reduce.2.cloned.1.call-start
  232.6 25.2 %reduce-scatter.2.cloned.1.call-done = f32[128,512]{1,0:T(8,128)} async-done(((f32[512,512]{1,0:T(8,128)}), f32[128,512]{1,0:T(8,128)}) %reduce-scatter.2.cloned.1.call-update) | async-done | bytes 262160 | tf_op jit(solution)/shard_map/reduce_scatter | solution.py:45
  257.7 0.0 all-reduce.2.cloned.1.call-update
  257.8 74.4 %all-reduce.2.cloned.1.call-done = f32[128,512]{1,0:T(8,128)} async-done(((f32[128,512]{1,0:T(8,128)}), f32[128,512]{1,0:T(8,128)}) %all-reduce.2.cloned.1.call-update) | async-done | bytes 262160 | tf_op jit(solution)/shard_map/psum | solution.py:46
  332.1 1.7 copy.32
  333.8 0.0 copy-done.1
  (7 shorter events, 0.1 us)
Async XLA Ops:
  6.5 11.6 %copy-start = (s32[64,16,16]{0,2,1:T(8,128)S(1)}, s32[64,16,16]{0,2,1:T(8,128)}, u32[]{:S(2)}) copy-start(s32[64,16,16]{0,2,1:T(8,128)} %param.7) | copy-start | bytes 196612
  6.5 251.2 %reduce-scatter.2.cloned.1.call-start = ((), (), s32[]{:S(2)}) async-start(), calls=%async_computation.2 | async-start | bytes 1310720 | tf_op jit(solution)/shard_map/reduce_scatter | solution.py:45
  39.4 12.6 %copy-start.2 = (bf16[64,64]{1,0:T(8,128)(2,1)S(1)}, bf16[64,64]{1,0:T(8,128)(2,1)}, u32[]{:S(2)}) copy-start(bf16[64,64]{1,0:T(8,128)(2,1)} %param.6) | copy-start | bytes 24580
  221.2 112.6 %copy-start.1 = (s32[64,16,16]{0,2,1:T(8,128)S(1)}, s32[64,16,16]{0,2,1:T(8,128)}, u32[]{:S(2)}) copy-start(s32[64,16,16]{0,2,1:T(8,128)} %param.7) | copy-start | bytes 196612
  232.5 99.6 %all-reduce.2.cloned.1.call-start = ((), (), s32[]{:S(2)}) async-start(), calls=%async_computation.3 | async-start | bytes 524288 | tf_op jit(solution)/shard_map/psum | solution.py:46
Sparse Core Ops, SparseCore 0:
  232.6 25.0 reduce-scatter.1
  261.1 70.9 all-reduce.1
where the time goes:
time: 343 us; the launch traced here: 341 us
  blocking collectives  109 us (32%)
  waiting for transfers between devices  99.6 us (29%)
  local copies, waits for them, and re-layouts  80 us (23%)
  matrix products  30.4 us (9%)
  between operations  13.5 us (4%)
  other arithmetic  7.89 us (2%)
    all_to_all x1, blocking collectives, per_device(): lax.all_to_all(outgoing, 'lay', split_axis=0, concat_axis=1, tiled=True)  101 us
    psum x1, waiting for transfers between devices, per_device(): return lax.psum(row_sums, 'blk')  74.4 us
    reshape x2, local copies, waits for them, and re-layouts, per_device(): inter.astype(jnp.bfloat16)  26.2 us
    reduce_scatter x1, waiting for transfers between devices, per_device(): lax.psum_scatter(partial_value, 'lay', scatter_dimension=0, tiled=True)  25.2 us
    unnamed x9, local copies, waits for them, and re-layouts  14.6 us
    select_n x1, local copies, waits for them, and re-layouts, per_device(): jnp.where(tile_mask > 0, three_centre, jnp.zeros_like(three_centre))  12.6 us
    all_to_all x1, local copies, waits for them, and re-layouts, per_device(): lax.all_to_all(outgoing, 'lay', split_axis=0, concat_axis=1, tiled=True)  12 us
    convert_element_type x1, local copies, waits for them, and re-layouts, per_device(): jnp.einsum('pq,qmn->pmn', metric, masked, preferred_element_type=jnp.floa...  11.3 us
  transfers between devices with their start and end apart: 2, of which 2 were waited for; matrix products, arithmetic and copies ran while one was open for 0% of the time, Pallas kernels for 0%

commit v1 on v0

--- a/solution.py
+++ b/solution.py
@@ -43,7 +43,7 @@
         moved, coeffs.reshape(group_size * row_count, ao_width), preferred_element_type=jnp.float32
     )
     row_sums = lax.psum_scatter(partial_value, "lay", scatter_dimension=0, tiled=True)
-    return lax.psum(row_sums, "blk")
+    return jnp.sum(lax.all_gather(row_sums, "blk"), axis=0)
 
 
 def solution(mesh):

time: 343 us -> 320 us (0.933)
  waiting for transfers between devices: 99.6 us -> 76.4 us
    psum x1 -> x0, waiting for transfers between devices: 74.4 us -> none  [per_device(): return lax.psum(row_sums, 'blk')]
    all_gather x0 -> x1, waiting for transfers between devices: none -> 51.2 us  [per_device(): return jnp.sum(lax.all_gather(row_sums, 'blk'), axis=0)]
    unnamed x9 -> x8, local copies, waits for them, and re-layouts: 14.6 us -> 13 us
where the time goes in v1:
time: 320 us; the launch traced here: 318 us
  blocking collectives  109 us (34%)
  local copies, waits for them, and re-layouts  78.3 us (24%)
  waiting for transfers between devices  76.4 us (24%)
  matrix products  30.4 us (10%)
  between operations  13.5 us (4%)
  other arithmetic  10.4 us (3%)
    all_to_all x1, blocking collectives, per_device(): lax.all_to_all(outgoing, 'lay', split_axis=0, concat_axis=1, tiled=True)  101 us
    all_gather x1, waiting for transfers between devices, per_device(): return jnp.sum(lax.all_gather(row_sums, 'blk'), axis=0)  51.2 us
    reshape x2, local copies, waits for them, and re-layouts, per_device(): inter.astype(jnp.bfloat16)  26.2 us
    reduce_scatter x1, waiting for transfers between devices, per_device(): lax.psum_scatter(partial_value, 'lay', scatter_dimension=0, tiled=True)  25.2 us
    unnamed x8, local copies, waits for them, and re-layouts  13 us
    select_n x1, local copies, waits for them, and re-layouts, per_device(): jnp.where(tile_mask > 0, three_centre, jnp.zeros_like(three_centre))  12.6 us
    all_to_all x1, local copies, waits for them, and re-layouts, per_device(): lax.all_to_all(outgoing, 'lay', split_axis=0, concat_axis=1, tiled=True)  12 us
    convert_element_type x1, local copies, waits for them, and re-layouts, per_device(): jnp.einsum('pq,qmn->pmn', metric, masked, preferred_element_type=jnp.floa...  11.3 us
  transfers between devices with their start and end apart: 2, of which 2 were waited for; matrix products, arithmetic and copies ran while one was open for 0% of the time, Pallas kernels for 0%

profile of v1, /device:TPU:0, one launch (start us, length us, event | category | flops | bytes accessed | tf_op | source)
XLA Modules:
  0.0 318.3 jit_solution(17004688668480662849)
XLA Ops:
  6.5 0.0 copy-start
  6.5 0.0 reduce-scatter.2.cloned.1.call-start
  6.6 1.0 copy.28
  7.7 1.7 gather_fusion.1
  9.4 0.1 copy.27
  9.5 8.7 %all_gather.9 = bf16[512,512]{0,1:T(8,128)(2,1)S(1)} all-gather(bf16[128,512]{0,1:T(8,128)(2,1)S(1)} %copy.28), channel_id=1, replica_groups=mesh['blk'=8,'lay'=4] {'lay'}, dimensions={0}, use_global_device_ids=true | all-gather | bytes 655360 | tf_op jit(solution)/shard_map/all_gather | solution.py:33
  18.2 0.0 copy-done
  18.2 0.8 gather_fusion
  18.9 0.3 fusion
  19.2 0.7 copy.23
  19.9 11.9 %copy.24 = bf16[64,128,512]{1,2,0:T(8,128)(2,1)} copy(bf16[64,128,512]{2,1,0:T(8,128)(2,1)} %param.5) | data formatting | bytes 16777216 | tf_op args[0]
  31.9 7.5 %bitcast_select_fusion = bf16[64,128,512]{1,2,0:T(8,128)(2,1)} fusion(bf16[64,128,512]{1,2,0:T(8,128)(2,1)} %copy.24, pred[64,128,16]{1,2,0:T(8,128)(4,1)S(1)} %copy.23), kind=kLoop, calls=%fused_computation.2 | loop fusion | flops 4194304 | bytes 16908288 | tf_op jit(solution)/shard_map/jit(_where)/select_n | solution.py:27
  39.4 0.0 copy-start.2
  39.4 12.6 %copy.25 = bf16[64,128,512]{2,0,1:T(8,128)(2,1)} copy(bf16[64,128,512]{1,2,0:T(8,128)(2,1)} %bitcast_select_fusion) | data formatting | bytes 16777216 | tf_op jit(solution)/shard_map/jit(_where)/select_n | solution.py:27
  52.0 0.0 copy-done.2
  52.0 8.9 %convert_bitcast_fusion = bf16[64,128,512]{2,0,1:T(8,128)(2,1)} fusion(bf16[64,128,512]{2,0,1:T(8,128)(2,1)} %copy.25, bf16[64,64]{1,0:T(8,128)(2,1)S(1)} %copy-done.2), kind=kOutput, calls=%fused_computation.4 | convolution fusion | flops 541065216 | bytes 16785408 | tf_op jit(solution)/shard_map/pq,qmn->pmn/dot_general | solution.py:28
  60.9 11.3 %copy.26 = bf16[64,128,512]{2,1,0:T(8,128)(2,1)} copy(bf16[64,128,512]{2,0,1:T(8,128)(2,1)} %convert_bitcast_fusion) | data formatting | bytes 16777216 | tf_op jit(solution)/shard_map/convert_element_type | solution.py:28
  72.2 0.1 bitcast_select_fusion.1
  72.3 10.2 %convolution_convert_fusion = bf16[8192,512]{1,0:T(8,128)(2,1)} fusion(bf16[8192,512]{1,0:T(8,128)(2,1)} %bitcast.26, bf16[512,512]{0,1:T(8,128)(2,1)S(1)} %bitcast_select_fusion.1), kind=kOutput, calls=%fused_computation.3 | convolution fusion | flops 4299161600 | bytes 17301504 | tf_op jit(solution)/shard_map/dot_general | solution.py:15
  82.5 12.5 %reshape.138 = bf16[64,128,4,128]{3,2,1,0:T(4,128)(2,1)} reshape(bf16[8192,512]{1,0:T(8,128)(2,1)} %convolution_convert_fusion) | data formatting | bytes 16777216 | tf_op jit(solution)/shard_map/reshape | solution.py:36
  95.0 13.6 %copy.29 = bf16[64,128,4,128]{1,3,0,2:T(8,128)(2,1)} copy(bf16[64,128,4,128]{3,2,1,0:T(4,128)(2,1)} %reshape.138) | data formatting | bytes 16777216 | tf_op jit(solution)/shard_map/reshape | solution.py:36
  108.7 100.6 %all_to_all.4 = bf16[4,128,8192]{1,2,0:T(8,128)(2,1)} all-to-all(bf16[4,128,8192]{1,2,0:T(8,128)(2,1)} %bitcast.25), channel_id=1, replica_groups=mesh['blk'=8,'lay'=4] {'lay'}, dimensions={0} | all-to-all | bytes 16777216 | tf_op jit(solution)/shard_map/all_to_all | solution.py:40
  209.2 12.0 %copy.30 = bf16[4,128,8192]{2,1,0:T(8,128)(2,1)} copy(bf16[4,128,8192]{1,2,0:T(8,128)(2,1)} %all_to_all.4) | data formatting | bytes 16777216 | tf_op jit(solution)/shard_map/all_to_all | solution.py:40
  221.2 0.0 copy-start.1
  221.2 11.3 %fusion.6 = f32[512,512]{1,0:T(8,128)} fusion(bf16[512,8192]{1,0:T(8,128)(2,1)} %bitcast.28, bf16[8192,512]{1,0:T(8,128)(2,1)} %bitcast.27), kind=kOutput, calls=%fused_computation.38 | convolution fusion | flops 4294967296 | bytes 17825792 | tf_op jit(solution)/shard_map/dot_general | solution.py:42
  232.5 0.0 reduce-scatter.2.cloned.1.call-update
  232.5 0.0 all-gather.3.cloned.1.call-start
  232.6 25.2 %reduce-scatter.2.cloned.1.call-done = f32[128,512]{1,0:T(8,128)} async-done(((f32[512,512]{1,0:T(8,128)}), f32[128,512]{1,0:T(8,128)}) %reduce-scatter.2.cloned.1.call-update) | async-done | bytes 262160 | tf_op jit(solution)/shard_map/reduce_scatter | solution.py:45
  257.7 0.0 all-gather.3.cloned.1.call-update
  257.8 51.2 %all-gather.3.cloned.1.call-done = f32[1024,512]{1,0:T(8,128)} async-done(((f32[128,512]{1,0:T(8,128)}), f32[1024,512]{1,0:T(8,128)}) %all-gather.3.cloned.1.call-update) | async-done | bytes 2097168 | tf_op jit(solution)/shard_map/all_gather | solution.py:46
  309.0 2.5 reduce_sum.9
  311.5 0.0 copy-done.1
  (7 shorter events, 0.1 us)
Async XLA Ops:
  6.5 11.6 %copy-start = (s32[64,16,16]{0,2,1:T(8,128)S(1)}, s32[64,16,16]{0,2,1:T(8,128)}, u32[]{:S(2)}) copy-start(s32[64,16,16]{0,2,1:T(8,128)} %param.7) | copy-start | bytes 196612
  6.5 251.2 %reduce-scatter.2.cloned.1.call-start = ((), (), s32[]{:S(2)}) async-start(), calls=%async_computation.2 | async-start | bytes 1310720 | tf_op jit(solution)/shard_map/reduce_scatter | solution.py:45
  39.4 12.6 %copy-start.2 = (bf16[64,64]{1,0:T(8,128)(2,1)S(1)}, bf16[64,64]{1,0:T(8,128)(2,1)}, u32[]{:S(2)}) copy-start(bf16[64,64]{1,0:T(8,128)(2,1)} %param.6) | copy-start | bytes 24580
  221.2 90.3 %copy-start.1 = (s32[64,16,16]{0,2,1:T(8,128)S(1)}, s32[64,16,16]{0,2,1:T(8,128)}, u32[]{:S(2)}) copy-start(s32[64,16,16]{0,2,1:T(8,128)} %param.7) | copy-start | bytes 196612
  232.5 76.5 %all-gather.3.cloned.1.call-start = ((), (), s32[]{:S(2)}) async-start(), calls=%async_computation.3 | async-start | bytes 2359296 | tf_op jit(solution)/shard_map/all_gather | solution.py:46
Sparse Core Ops, SparseCore 0:
  232.6 25.0 reduce-scatter.1
  259.9 49.0 all-gather.2
